TPU v7x, 32 devices: a whole 2x2x4 slice. The times are simulated.
32 devices in a mesh: seq: 16 (over z, y, core), dp: 2 (over x).
Axes of the slice: x: 2, y: 2, z: 4, core: 2. Of those that a mesh axis runs over, the one named last changes fastest.
Arguments:
- acceptors: bfloat16 [2, 2048, 2560], P('dp', 'seq'), may hold values from -2 to 2
- lookups: bfloat16 [2, 2048, 2560], P('dp', 'seq'), may hold values from -0.625 to 0.625
- payloads: bfloat16 [2, 2048, 2560], P('dp', 'seq'), may hold values from -6 to 6
- lagged_fading_source: bfloat16 [2, 2048, 2560], P('dp', 'seq'), may hold values from -6 to 6
- response_cotangent: bfloat16 [2, 2048, 2560], P('dp', 'seq'), may hold values from -5 to 5
- fading_lowering_array: bfloat16 [2560, 128], replicated, may hold values from -0.125 to 0.125
- fading_raising_array: bfloat16 [2560, 128], replicated, may hold values from -1.25 to 1.25
- feature_fading_speed: float32 [2560], replicated, may hold values from 2.3251488e-05 to 0.125
- present_reward: float32 [2560], replicated, may hold values from 1.4142135 to 11.313708
Outputs:
- mixed: bfloat16 [2, 2048, 2560], P('dp', 'seq')
- grad_receptance: bfloat16 [2, 2048, 2560], P('dp', 'seq')
- lookup_deriv: bfloat16 [2, 2048, 2560], P('dp', 'seq')
- payload_deriv: bfloat16 [2, 2048, 2560], P('dp', 'seq')
- grad_decay_input: bfloat16 [2, 2048, 2560], P('dp', 'seq')
- grad_lora_a: float32 [2560, 128], P('dp')
- grad_lora_b: float32 [2560, 128], P('dp')
- grad_time_decay: float32 [2560], P('dp')
- present_reward_deriv: float32 [2560], P('dp')
All inputs are finite; a program needn't handle non-finite values.
Results may differ from a plain program's by a relative error of at most 0.006.
Values sent between devices are 32-bit elements.
A program may use at most 320 MiB of HBM per device.

v0:
```python
import jax
import jax.numpy as jnp
from jax import lax
from jax.sharding import PartitionSpec as P

ATTENDER_TOTAL = 40
LANE_TOTAL = 64
BLOCK = 64
HIGH = lax.Precision.HIGHEST


def carried_in(part, axis, combine, identity, reverse):
    count = lax.axis_size(axis)
    place = lax.axis_index(axis)
    ahead = count - 1 - place if reverse else place
    gathered = jax.tree.map(lambda a: lax.all_gather(a, axis), part)
    state = jax.tree.map(lambda a, e: jnp.zeros_like(a) + jnp.asarray(e, a.dtype), part, identity)

    def one(hop, state):
        source = count - 1 - hop if reverse else hop
        return combine(
            state, jax.tree.map(lambda a: lax.dynamic_index_in_dim(a, source, 0, False), gathered)
        )

    return lax.fori_loop(0, ahead, one, state)


def contract(pattern, left, right):
    return jnp.einsum(pattern, left, right, precision=HIGH, preferred_element_type=jnp.float32)


def decay_log_values(input_rows, fading_lowering_array, fading_raising_array, feature_fading_speed):
    apply_projection = jnp.dot(
        input_rows, fading_lowering_array, preferred_element_type=jnp.float32
    )
    smoothed_values = jnp.tanh(apply_projection)
    gate_portion = smoothed_values.astype(jnp.bfloat16)
    rank_projection = lax.dot_general(
        gate_portion,
        fading_raising_array,
        (((1,), (1,)), ((), ())),
        preferred_element_type=jnp.float32,
    )
    return (
        smoothed_values,
        gate_portion,
        -feature_fading_speed[None, :] * jnp.exp(rank_projection),
    )


def compose(decays, own_states, backward):

    def advance(carry, member):
        run_decay, run_state = carry
        decay, own_state = member
        return ((run_decay * decay, decay[..., None] * run_state + own_state), carry)

    initial = (
        jnp.ones(decays.shape[1:], jnp.float32),
        jnp.zeros(own_states.shape[1:], jnp.float32),
    )
    return lax.scan(advance, initial, (decays, own_states), reverse=backward)


def follow(earlier, later):
    return (earlier[0] * later[0], later[0][..., None] * earlier[1] + later[1])


def temporal_blend_sublevel(
    acceptor_lines,
    lookups,
    payloads,
    incoming_cotangent,
    fading_exponent,
    reward_by_attender,
    adjacent_shardlink,
):
    inclusive = jnp.cumsum(fading_exponent, axis=1)
    exclusive = inclusive - fading_exponent
    middle = inclusive[:, BLOCK // 2 - 1 : BLOCK // 2]
    overall = inclusive[:, -1]
    entering = jnp.exp(exclusive)
    leaving = jnp.exp(overall[:, None] - inclusive)
    upward = jnp.exp(exclusive - middle)
    downward = jnp.exp(middle - inclusive)
    decays = jnp.exp(overall)
    reached = acceptor_lines * entering
    faded_keys = lookups * leaving
    own_states = contract("nchk,nchv->nhkv", faded_keys, payloads)
    pull_states = contract("nchk,nchv->nhkv", reached, incoming_cotangent)
    starts, block_ends = adjacent_shardlink(decays, own_states, pull_states)
    position = jnp.arange(BLOCK)
    beneath = position[:, None] > position[None, :]
    early_recept = acceptor_lines * upward
    late_keys = lookups * downward
    scores = jnp.where(beneath, contract("nthk,nshk->nhts", early_recept, late_keys), 0.0)
    present_contribution = jnp.sum(acceptor_lines * reward_by_attender * lookups, axis=-1)[
        ..., None
    ]
    blended_response = (
        contract("nhts,nshv->nthv", scores, payloads)
        + present_contribution * payloads
        + contract("nthk,nhkv->nthv", reached, starts)
    )
    grad_start = decays[..., None] * block_ends + pull_states
    products = jnp.where(beneath, contract("nthv,nshv->nhts", incoming_cotangent, payloads), 0.0)
    agreement_verify = jnp.sum(payloads * incoming_cotangent, axis=-1)[..., None]
    memory_acceptors = entering * contract(
        "nhkv,nthv->nthk", starts, incoming_cotangent
    ) + upward * contract("nhts,nshk->nthk", products, late_keys)
    memory_lookup_lines = leaving * contract(
        "nhkv,nthv->nthk", block_ends, payloads
    ) + downward * contract("nhst,nshk->nthk", products, early_recept)
    payload_deriv = (
        contract("nthk,nhkv->nthv", faded_keys, block_ends)
        + contract("nhst,nshv->nthv", scores, incoming_cotangent)
        + present_contribution * incoming_cotangent
    )
    acceptor_deriv = memory_acceptors + reward_by_attender * lookups * agreement_verify
    lookup_deriv = memory_lookup_lines + reward_by_attender * acceptor_lines * agreement_verify
    present_reward_deriv = jnp.sum(acceptor_lines * lookups * agreement_verify, axis=(0, 1))
    coupling = jnp.sum(grad_start * starts, axis=-1)
    change = lookups * memory_lookup_lines - acceptor_lines * memory_acceptors
    fading_deriv = (
        coupling[:, None] + jnp.cumsum(change, axis=1) - change - acceptor_lines * memory_acceptors
    )
    return (
        blended_response,
        acceptor_deriv,
        lookup_deriv,
        payload_deriv,
        fading_deriv,
        present_reward_deriv,
    )


def sublevel_evaluation(
    reshaped_acceptors,
    reshaped_lookups,
    reshaped_payloads,
    reshaped_source,
    incoming_cotangent_reshaped,
    fading_lowering_array,
    fading_raising_array,
    feature_fading_speed,
    present_reward,
    adjacent_shardlink,
):
    smoothed_values, gate_portion, fading_exponent = decay_log_values(
        reshaped_source, fading_lowering_array, fading_raising_array, feature_fading_speed
    )
    tokens, feature_span = reshaped_acceptors.shape
    tiling_arrangement = (tokens // BLOCK, BLOCK, ATTENDER_TOTAL, LANE_TOTAL)
    collected_outcomes = temporal_blend_sublevel(
        reshaped_acceptors.astype(jnp.float32).reshape(tiling_arrangement),
        reshaped_lookups.astype(jnp.float32).reshape(tiling_arrangement),
        reshaped_payloads.astype(jnp.float32).reshape(tiling_arrangement),
        incoming_cotangent_reshaped.astype(jnp.float32).reshape(tiling_arrangement),
        fading_exponent.reshape(tiling_arrangement),
        present_reward.reshape(ATTENDER_TOTAL, LANE_TOTAL),
        adjacent_shardlink,
    )
    (
        blended_response,
        acceptor_deriv,
        lookup_deriv,
        payload_deriv,
        fading_deriv,
        present_reward_deriv,
    ) = collected_outcomes
    slope = fading_deriv.reshape(tokens, feature_span) * fading_exponent
    slope_portion = slope.astype(jnp.bfloat16)
    gate_gradient = jnp.dot(slope_portion, fading_raising_array, preferred_element_type=jnp.float32)
    projection_gradient = (gate_gradient * (1.0 - smoothed_values * smoothed_values)).astype(
        jnp.bfloat16
    )
    input_gradient = lax.dot_general(
        projection_gradient,
        fading_lowering_array,
        (((1,), (1,)), ((), ())),
        preferred_element_type=jnp.float32,
    ).astype(jnp.bfloat16)
    lowering_array_deriv = lax.dot_general(
        reshaped_source,
        projection_gradient,
        (((0,), (0,)), ((), ())),
        preferred_element_type=jnp.float32,
    )
    raising_array_deriv = lax.dot_general(
        slope_portion, gate_portion, (((0,), (0,)), ((), ())), preferred_element_type=jnp.float32
    )
    speed_deriv = jnp.sum(slope, axis=0)

    def flatten(member):
        return member.reshape(tokens, feature_span).astype(jnp.bfloat16)

    return (
        flatten(blended_response),
        flatten(acceptor_deriv),
        flatten(lookup_deriv),
        flatten(payload_deriv),
        input_gradient,
        (
            lowering_array_deriv,
            raising_array_deriv,
            speed_deriv,
            present_reward_deriv.reshape(feature_span),
        ),
    )


def shard_link(decays, own_states, pull_states):
    ahead_total, ahead = compose(decays, own_states, False)
    behind_total, behind = compose(decays, pull_states, True)
    identity = (jnp.ones_like(ahead_total[0]), jnp.zeros_like(ahead_total[1]))
    prior, state_in = carried_in(ahead_total, "seq", follow, identity, False)
    latter, grad_after = carried_in(behind_total, "seq", follow, identity, True)
    starts = ahead[0][..., None] * state_in[None] + ahead[1]
    block_ends = behind[0][..., None] * grad_after[None] + behind[1]
    return (starts, block_ends)


def per_device(
    acceptors,
    lookups,
    payloads,
    lagged_fading_source,
    response_cotangent,
    fading_lowering_array,
    fading_raising_array,
    feature_fading_speed,
    present_reward,
):
    collected_outcomes = sublevel_evaluation(
        acceptors[0],
        lookups[0],
        payloads[0],
        lagged_fading_source[0],
        response_cotangent[0],
        fading_lowering_array,
        fading_raising_array,
        feature_fading_speed,
        present_reward,
        shard_link,
    )
    sums = collected_outcomes[5]
    dp_count = lax.axis_size("dp")
    share_rows = fading_lowering_array.shape[0] // dp_count
    whole = lax.psum((sums[0], sums[1], sums[2], sums[3]), ("seq", "dp"))
    offset = lax.axis_index("dp") * share_rows
    reduced = tuple((lax.dynamic_slice_in_dim(member, offset, share_rows, 0) for member in whole))
    return (
        collected_outcomes[0][None],
        collected_outcomes[1][None],
        collected_outcomes[2][None],
        collected_outcomes[3][None],
        collected_outcomes[4][None],
        reduced[0],
        reduced[1],
        reduced[2],
        reduced[3],
    )


def solution(mesh):
    in_specs = (
        P("dp", "seq", None),
        P("dp", "seq", None),
        P("dp", "seq", None),
        P("dp", "seq", None),
        P("dp", "seq", None),
        P(),
        P(),
        P(),
        P(),
    )
    out_specs = (
        P("dp", "seq", None),
        P("dp", "seq", None),
        P("dp", "seq", None),
        P("dp", "seq", None),
        P("dp", "seq", None),
        P("dp", None),
        P("dp", None),
        P("dp"),
        P("dp"),
    )
    return jax.shard_map(
        per_device, mesh=mesh, in_specs=in_specs, out_specs=out_specs, check_vma=False
    )
```

profile of v0, /device:TPU:0, one launch (start us, length us, event | category | flops | bytes accessed | tf_op | source)
XLA Modules:
  0.0 555.1 jit_solution(3904437213683768561)
XLA Ops:
  19.8 2.9 reshape.128
  22.7 3.2 copy.93
  28.6 5.5 fusion.57
  36.0 17.7 %while.66 = (s32[]{:T(128)}, f32[40,64]{1,0:T(8,128)S(1)}, f32[40,64,64]{2,1,0:T(8,128)}, f32[2,40,64]{2,1,0:T(8,128)S(1)}, f32[2,40,64,64]{2,3,1,0:T(8,128)}, /...) while((s32[]{:T(128)}, f32[40,64]{1,0:T(8,128)S(1)}, ...), condition=%wide.region_3.4_spmd.clone, body=%wide.region_2.3_spmd.clone.sunk | while | flops 499203 | bytes 6646389 | solution.py:62
  36.0 3.2 select_bitcast_fusion.4
  39.3 2.8 copy.180
  44.6 3.6 select_bitcast_fusion.4
  48.3 2.8 copy.180
  53.9 3.3 copy.90
  59.8 2.8 reshape.127
  62.6 3.6 copy.91
  66.2 7.1 %fusion.50 = f32[2,40,64,64]{2,3,1,0:T(8,128)} fusion(f32[2,64,40,64]{1,3,2,0:T(8,128)} %copy.91, bf16[2,64,40,64]{3,2,1,0:T(8,128)(2,1)} %reshape.125, f32[2,64,40,64]{1,3,2,0:T(8,128)S(1)} %copy.89, f32[2,64,40,64]{1,3,2,0:T(8,128)} %copy.90), kind=kOutput, calls=%fused_computation.85 | convolution fusion | flops 252313600 | bytes 5898240 | tf_op jit(solution)/shard_map/nchk,nchv->nhkv/dot_general | solution.py:29
  75.7 29.7 %while.67 = (s32[]{:T(128)}, f32[40,64]{1,0:T(8,128)S(1)}, f32[40,64,64]{2,1,0:T(8,128)}, f32[2,40,64]{2,1,0:T(8,128)}, f32[2,40,64,64]{2,3,1,0:T(8,128)}, /*ind...) while((s32[]{:T(128)}, f32[40,64]{1,0:T(8,128)S(1)}, ...), condition=%wide.region_8.9_spmd.clone, body=%wide.region_7.8_spmd.clone.sunk | while | flops 499204 | bytes 9257093 | solution.py:62
  76.3 2.7 constant_dynamic-slice_fusion.4
  79.0 2.8 copy.181
  81.8 3.3 select_bitcast_fusion.5
  85.0 2.8 copy.182
  93.6 2.8 copy.181
  96.4 3.7 select_bitcast_fusion.5
  100.1 2.8 copy.182
  106.3 3.1 fusion.5
  110.8 2.7 mul.266.clone
  113.5 2.9 mul.285
  116.3 27.7 %all-gather = f32[640,64]{1,0:T(8,128)} all-gather(f32[40,64]{1,0:T(8,128)S(1)} %get-tuple-element.322), channel_id=2, replica_groups=mesh['seq'=16,'dp'=2] {'seq'}, dimensions={0}, use_global_device_ids=true | all-gather | bytes 174080 | tf_op jit(solution)/shard_map/all_gather | solution.py:16
  144.0 21.9 %all-gather.2 = f32[640,64]{1,0:T(8,128)} all-gather(f32[40,64]{1,0:T(8,128)S(1)} %get-tuple-element.327), channel_id=4, replica_groups=mesh['seq'=16,'dp'=2] {'seq'}, dimensions={0}, use_global_device_ids=true | all-gather | bytes 174080 | tf_op jit(solution)/shard_map/all_gather | solution.py:16
  166.0 2.8 multiply_reduce_fusion.2
  168.8 4.1 fusion.62
  172.9 7.7 %fusion.52 = f32[2,40,64,64]{3,2,1,0:T(8,128)} fusion(f32[2,64,40,64]{1,3,2,0:T(8,128)S(1)} %copy-done.3, f32[2,64,40,64]{1,3,2,0:T(8,128)S(1)} %copy.89, f32[2,40,64]{2,1,0:T(8,128)S(1)} %get-tuple-element.494, f32[2,64,40,64]{1,3,2,0:T(8,128)S(1)} %copy-done.6, f32[2,64,40,64]{1,3,2,0:T(8,128)S(1)} %copy-done.1), kind=kOutput, calls=%fused_computation.86 | convolution fusion | flops 253296640 | bytes 6574080 | tf_op jit(solution)/shard_map/nthk,nshk->nhts/dot_general | solution.py:29
  182.0 2.8 copy.103
  184.8 97.0 %all-gather.9.cloned.1.call-done = f32[640,64,64]{2,1,0:T(8,128)} async-done(((f32[40,64,64]{2,1,0:T(8,128)}), f32[640,64,64]{2,1,0:T(8,128)}) %all-gather.9.cloned.1.call-update) | async-done | bytes 10485776 | tf_op jit(solution)/shard_map/all_gather | solution.py:16
  283.1 60.2 %while.65 = (s32[]{:T(128)}, f32[40,64,64]{2,1,0:T(8,128)}, s32[]{:T(128)}, f32[16,40,64]{2,1,0:T(8,128)}, f32[16,40,64,64]{3,2,1,0:T(8,128)}, /*index=5*/s32[]{:T(128)}, s32[]{:T(128)}, s32[]{:T(128)}, s32[]{:T(128)}) while((s32[]{:T(128)}, f32[40,64,64]{2,1,0:T(8,128)}, s32[]{:T(128)}, f32[16,40,64]{2,1,0:T(8,128)}, ...), condition=%wide.region_10.11_spmd, body=%wide.region_9.10_spmd.sunk | while | flops 327686 | bytes 1996947 | solution.py:25
  283.8 3.3 bitcast_add_fusion.8
  287.8 3.3 bitcast_add_fusion.8
  291.8 3.3 bitcast_add_fusion.8
  295.8 3.3 bitcast_add_fusion.8
  299.8 3.3 bitcast_add_fusion.8
  303.9 3.3 bitcast_add_fusion.8
  307.9 3.3 bitcast_add_fusion.8
  311.9 3.3 bitcast_add_fusion.8
  315.9 3.3 bitcast_add_fusion.8
  319.9 3.3 bitcast_add_fusion.8
  323.9 3.3 bitcast_add_fusion.8
  327.9 3.3 bitcast_add_fusion.8
  331.9 3.3 bitcast_add_fusion.8
  335.9 3.3 bitcast_add_fusion.8
  339.9 3.3 bitcast_add_fusion.8
  343.2 2.8 copy.119
  346.1 6.4 %fusion.24 = f32[2,40,64,64]{3,2,1,0:T(8,128)} fusion(f32[2,40,64,64]{2,3,1,0:T(8,128)} %get-tuple-element.330, f32[40,64,64]{1,2,0:T(8,128)} %copy.119, f32[2,40,64]{2,1,0:T(8,128)S(1)} %copy-done.23, bf16[2,64,40,64]{3,2,1,0:T(8,128)(2,1)} %reshape.124), kind=kOutput, calls=%fused_computation.64 | convolution fusion | flops 252313600 | bytes 3952640 | tf_op jit(solution)/shard_map/nhkv,nthv->nthk/dot_general | solution.py:29
  352.5 4.1 multiply_reduce_fusion
  359.9 6.5 %fusion.9 = f32[2,64,40,64]{1,3,2,0:T(8,128)} fusion(f32[2,40,64,64]{3,2,1,0:T(8,128)S(1)} %fusion.21, f32[2,40,64,64]{3,2,1,0:T(8,128)S(1)} %copy-done.16, f32[2,40,64]{2,1,0:T(8,128)S(1)} %get-tuple-element.494, pred[64,64]{1,0:T(8,128)(4,1)S(1)} %iota_compare_fusion, f32[2,64,40,64]{1,3,2,0:T(8,128)S(1)} %copy-done.4, f32[2,64,40,64]{1,3,2,0:T(8,128)S(1)} %copy.89, ...), kind=kOutput, calls=%fused_computation.36 | convolution fusion | flops 254279680 | bytes 7888896 | tf_op jit(solution)/shard_map/nhts,nshk->nthk/dot_general | solution.py:29
  366.4 11.1 %multiply_subtract_fusion = (f32[2,64,40,64]{1,3,2,0:T(8,128)}, f32[2,64,40,64]{1,3,2,0:T(8,128)}, bf16[2,64,40,64]{1,3,2,0:T(8,128)(2,1)}, bf16[2,64,40,64]{1,3,2,0:T(8,128)(2,1)}, f32[2,64,40]{1,2,0:T(8,128)}) fusion(f32[2,64,40,64]{1,3,2,0:T(8,128)S(1)} %copy-done.4, f32[2,64,40,64]{1,3,2,0:T(8,128)S(1)} %copy-done.7, f32[2,64,40,64]{1,3,2,0:T(8,128)} %fusion.9, ...), kind=kOutput, calls=%fused_computation.39 | convolution fusion | flops 258862080 | bytes 13203456 | tf_op jit(solution)/shard_map/nhst,nshk->nthk/dot_general | solution.py:29
  377.5 3.2 copy.131
  380.7 3.5 fusion.83
  384.2 3.2 copy.132
  387.4 5.0 subtract_subtract_fusion
  392.4 3.3 copy.133
  395.7 3.2 reshape.126
  403.0 6.6 %fusion.23 = f32[2,40,64,64]{2,3,1,0:T(8,128)} fusion(f32[2,40,64,64]{2,3,1,0:T(8,128)S(1)} %copy-done.13, f32[40,64,64]{1,2,0:T(8,128)S(1)} %copy-done.18, f32[2,40,64]{2,1,0:T(8,128)S(1)} %copy-done.24, f32[2,64,40,64]{1,3,2,0:T(8,128)S(1)} %copy-done.5, f32[2,64,40,64]{1,3,2,0:T(8,128)S(1)} %copy.89, f32[2,40,64]{2,1,0:T(8,128)S(1)} %copy-done.22), kind=kOutput, calls=%fused_computation.63 | convolution fusion | flops 252968960 | bytes 5939200 | tf_op jit(solution)/shard_map/nthk,nhkv->nthv/dot_general | solution.py:29
  411.1 7.4 %fusion.7 = bf16[2,64,40,64]{3,1,2,0:T(8,128)(2,1)} fusion(f32[2,40,64,64]{2,3,1,0:T(8,128)} %fusion.23, f32[2,40,64,64]{3,2,1,0:T(8,128)} %fusion.52, f32[2,64,40]{1,2,0:T(8,128)S(1)} %copy-done.26, pred[64,64]{1,0:T(8,128)(4,1)S(1)} %iota_compare_fusion, bf16[2,64,40,64]{3,2,1,0:T(8,128)(2,1)} %reshape.125), kind=kOutput, calls=%fused_computation.30 | convolution fusion | flops 253624320 | bytes 3956736 | tf_op jit(solution)/shard_map/nhst,nshv->nthv/dot_general | solution.py:29
  418.6 37.4 %all-reduce = (f32[2560]{0:T(1024)S(1)}, f32[2560]{0:T(1024)S(1)}) all-reduce(f32[2560]{0:T(1024)S(1)} %get-tuple-element.492, f32[2560]{0:T(1024)S(1)} %copy-done.29), channel_id=1, replica_groups=mesh['seq'=16,'dp'=2] {'seq','dp'}, use_global_device_ids=true, to_apply=%region_16.17 | all-reduce | flops 5120 | bytes 40960 | tf_op jit(solution)/shard_map/psum | solution.py:249
  457.3 3.2 copy.128
  460.6 2.8 convert_element_type.122
  463.3 8.7 %fusion.22 = f32[2,40,64,64]{2,3,1,0:T(8,128)S(1)} fusion(f32[2,40,64,64]{2,3,1,0:T(8,128)} %get-tuple-element.325, f32[40,64,64]{1,2,0:T(8,128)} %copy.103, f32[2,40,64]{2,1,0:T(8,128)S(1)} %get-tuple-element.321, f32[2,64,40,64]{1,3,2,0:T(8,128)} %copy.91, f32[2,64,40,64]{1,3,2,0:T(8,128)S(1)} %copy.89, f32[2,64,40,64]{1,3,2,0:T(8,128)} %copy.90), kind=kOutput, calls=%fused_computation.62 | convolution fusion | flops 252968960 | bytes 7229440 | tf_op jit(solution)/shard_map/nthk,nhkv->nthv/dot_general | solution.py:29
  485.3 59.9 %all-reduce.4.cloned.1.call-done = (f32[2560,128]{0,1:T(8,128)}, f32[2560,128]{1,0:T(8,128)}) async-done(((f32[2560,128]{0,1:T(8,128)}, f32[2560,128]{1,0:T(8,128)}), (f32[2560,128]{0,1:T(8,128)}, f32[2560,128]{1,0:T(8,128)})) %all-reduce.4.cloned.1.call-update) | async-done | bytes 2621456 | tf_op jit(solution)/shard_map/psum | solution.py:249
  (137 shorter events, 78.9 us)
Async XLA Ops:
  7.2 2.4 copy-start
  7.2 173.4 %all-gather.7.cloned.1.call-start = ((), (), s32[]{:S(2)}) async-start(), calls=%async_computation | async-start | bytes 22282240 | tf_op jit(solution)/shard_map/all_gather | solution.py:16
  12.8 1.5 copy-start.14
  18.9 9.7 %copy-start.21 = (f32[2,40,64]{2,1,0:T(8,128)}, f32[2,40,64]{2,1,0:T(8,128)S(1)}, u32[]{:S(2)}) copy-start(f32[2,40,64]{2,1,0:T(8,128)S(1)} %get-tuple-element.495) | copy-start | bytes 61444
  53.7 228.2 %all-gather.9.cloned.1.call-start = ((), (), s32[]{:S(2)}) async-start(), calls=%async_computation.1 | async-start | bytes 22282240 | tf_op jit(solution)/shard_map/all_gather | solution.py:16
  105.4 439.8 %all-reduce.4.cloned.1.call-start = ((), (), s32[]{:S(2)}) async-start(), calls=%async_computation.2 | async-start | bytes 5242880 | tf_op jit(solution)/shard_map/psum | solution.py:249
  166.0 6.9 %copy-start.6 = (f32[2,64,40,64]{1,3,2,0:T(8,128)S(1)}, f32[2,64,40,64]{1,3,2,0:T(8,128)}, u32[]{:S(2)}) copy-start(f32[2,64,40,64]{1,3,2,0:T(8,128)} %copy.91) | copy-start | bytes 3932164
  168.8 4.1 copy-start.1
  168.8 4.1 copy-start.3
  343.2 2.8 copy-start.23
  346.0 6.4 %copy-start.8 = (f32[2,40,64,64]{2,3,1,0:T(8,128)S(1)}, f32[2,40,64,64]{2,3,1,0:T(8,128)}, u32[]{:S(2)}) copy-start(f32[2,40,64,64]{2,3,1,0:T(8,128)} %get-tuple-element.773) | copy-start | bytes 3932164
  346.0 6.4 %copy-start.11 = (f32[2,40,64,64]{2,3,1,0:T(8,128)S(1)}, f32[2,40,64,64]{2,3,1,0:T(8,128)}, u32[]{:S(2)}) copy-start(f32[2,40,64,64]{2,3,1,0:T(8,128)} %get-tuple-element.325) | copy-start | bytes 3932164
  346.0 6.4 %copy-start.12 = (f32[2,40,64,64]{2,3,1,0:T(8,128)S(1)}, f32[2,40,64,64]{2,3,1,0:T(8,128)}, u32[]{:S(2)}) copy-start(f32[2,40,64,64]{2,3,1,0:T(8,128)} %get-tuple-element.330) | copy-start | bytes 3932164
  352.5 4.1 copy-start.10
  352.5 4.1 copy-start.17
  356.6 2.4 copy-start.2
  356.6 2.5 copy-start.4
  356.6 3.3 copy-start.16
  359.9 6.5 %copy-start.7 = (f32[2,64,40,64]{1,3,2,0:T(8,128)S(1)}, f32[2,64,40,64]{1,3,2,0:T(8,128)}, u32[]{:S(2)}) copy-start(f32[2,64,40,64]{1,3,2,0:T(8,128)} %copy.91) | copy-start | bytes 3932164
  359.9 6.5 %copy-start.22 = (f32[2,40,64]{2,1,0:T(8,128)S(1)}, f32[2,40,64]{2,1,0:T(8,128)}, u32[]{:S(2)}) copy-start(f32[2,40,64]{2,1,0:T(8,128)} %copy-done.21) | copy-start | bytes 61444
  359.9 6.5 %copy-start.25 = (f32[2,64,40]{1,2,0:T(8,128)S(1)}, f32[2,64,40]{1,2,0:T(8,128)}, u32[]{:S(2)}) copy-start(f32[2,64,40]{1,2,0:T(8,128)} %fusion.5) | copy-start | bytes 61444
  384.2 3.2 copy-start.28
  398.9 3.9 copy-start.5
  398.9 3.9 copy-start.13
  398.9 4.1 copy-start.18
  398.9 4.1 copy-start.24
  403.0 6.6 %copy-start.20 = (bf16[1,128,2560]{2,1,0:T(8,128)(2,1)S(1)}, bf16[1,128,2560]{2,1,0:T(8,128)(2,1)}, u32[]{:S(2)}) copy-start(bf16[1,128,2560]{2,1,0:T(8,128)(2,1)} %param.20) | copy-start | bytes 1966084
  409.7 1.4 copy-start.26
  411.1 7.5 %copy-start.29 = (f32[2560]{0:T(1024)S(1)}, f32[2560]{0:T(1024)}, u32[]{:S(2)}) copy-start(f32[2560]{0:T(1024)} %multiply_reduce_fusion.2) | copy-start | bytes 30724
  463.3 8.7 %copy-start.9 = (bf16[2,64,40,64]{3,2,1,0:T(8,128)(2,1)S(1)}, bf16[2,64,40,64]{3,2,1,0:T(8,128)(2,1)}, u32[]{:S(2)}) copy-start(bf16[2,64,40,64]{3,2,1,0:T(8,128)(2,1)} %reshape.124) | copy-start | bytes 1966084
  463.3 8.7 %copy-start.15 = (f32[2,40,64,64]{3,2,1,0:T(8,128)S(1)}, f32[2,40,64,64]{3,2,1,0:T(8,128)}, u32[]{:S(2)}) copy-start(f32[2,40,64,64]{3,2,1,0:T(8,128)} %fusion.52) | copy-start | bytes 3932164
  476.9 3.6 copy-start.19
  545.2 2.3 copy-start.27
Sparse Core Ops, SparseCore 0:
  53.8 117.4 all-gather.6
  172.8 108.9 all-gather.8
  411.2 133.9 all-reduce.3
where the time goes:
time: 564 us; the launch traced here: 555 us
  waiting for transfers between devices  157 us (28%)
  local copies, waits for them, and re-layouts  125 us (22%)
  other arithmetic  87.2 us (15%)
  blocking collectives  87 us (15%)
  matrix products  84.5 us (15%)
  between operations  14.3 us (3%)
    all_gather x2, waiting for transfers between devices, carried_in(): gathered = jax.tree.map(lambda a: lax.all_gather(a, axis), part)  97 us
    dot_general x12, matrix products, contract(): jnp.einsum(pattern, left, right, precision=HIGH, preferred_element_type=j...  76 us
    psum x1, waiting for transfers between devices, per_device(): whole = lax.psum((sums[0], sums[1], sums[2], sums[3]), ('seq', 'dp'))  59.9 us
    all_gather x2, blocking collectives, carried_in(): gathered = jax.tree.map(lambda a: lax.all_gather(a, axis), part)  49.6 us
    add x15, other arithmetic, follow(): return (earlier[0] * later[0], later[0][..., None] * earlier[1] + later[1])  49.2 us
    psum x1, blocking collectives, per_device(): whole = lax.psum((sums[0], sums[1], sums[2], sums[3]), ('seq', 'dp'))  37.4 us
    dynamic_update_slice x8, local copies, waits for them, and re-layouts, compose(): return lax.scan(advance, initial, (decays, own_states), reverse=backward)  21.4 us
    convert_element_type x8, local copies, waits for them, and re-layouts, flatten(): return member.reshape(tokens, feature_span).astype(jnp.bfloat16)  14.5 us
  transfers between devices with their start and end apart: 3, of which 2 were waited for; matrix products, arithmetic and copies ran while one was open for 21% of the time, Pallas kernels for 0%

commit v1 on v0

--- a/solution.py
+++ b/solution.py
@@ -246,7 +246,12 @@
     sums = collected_outcomes[5]
     dp_count = lax.axis_size("dp")
     share_rows = fading_lowering_array.shape[0] // dp_count
-    whole = lax.psum((sums[0], sums[1], sums[2], sums[3]), ("seq", "dp"))
+
+    def step_on_yards(panel, peer_axis, lane_axis):
+        base_arr = lax.psum(panel, peer_axis)
+        return lax.psum(base_arr, lane_axis)
+
+    whole = step_on_yards((sums[0], sums[1], sums[2], sums[3]), "seq", "dp")
     offset = lax.axis_index("dp") * share_rows
     reduced = tuple((lax.dynamic_slice_in_dim(member, offset, share_rows, 0) for member in whole))
     return (

time: 564 us -> 649 us (1.15)
  waiting for transfers between devices: 157 us -> 207 us
  blocking collectives: 87 us -> 129 us
    psum x1 -> x2, blocking collectives: 37.4 us -> 78.8 us  [the longest x1 58.1 us: step_on_yards(): base_arr = lax.psum(panel, peer_axis)]
    psum x1 -> x2, waiting for transfers between devices: 59.9 us -> 91 us  [the longest x1 91 us: step_on_yards(): base_arr = lax.psum(panel, peer_axis)]
    all_gather x2, waiting for transfers between devices: 97 us -> 116 us  [carried_in(): gathered = jax.tree.map(lambda a: lax.all_gather(a, axis), part)]
  transfers between devices with their start and end apart: 3 -> 4, of which waited for: 2 -> 3; matrix products, arithmetic and copies ran while one was open for 21% -> 18% of each run, Pallas kernels for 0% -> 0%
where the time goes in v1:
time: 649 us; the launch traced here: 640 us
  waiting for transfers between devices  207 us (32%)
  blocking collectives  129 us (20%)
  local copies, waits for them, and re-layouts  122 us (19%)
  other arithmetic  86 us (13%)
  matrix products  81.6 us (13%)
  between operations  14.3 us (2%)
    all_gather x2, waiting for transfers between devices, carried_in(): gathered = jax.tree.map(lambda a: lax.all_gather(a, axis), part)  116 us
    psum x1, waiting for transfers between devices, step_on_yards(): base_arr = lax.psum(panel, peer_axis)  91 us
    dot_general x12, matrix products, contract(): jnp.einsum(pattern, left, right, precision=HIGH, preferred_element_type=j...  73.1 us
    psum x1, blocking collectives, step_on_yards(): base_arr = lax.psum(panel, peer_axis)  58.1 us
    all_gather x2, blocking collectives, carried_in(): gathered = jax.tree.map(lambda a: lax.all_gather(a, axis), part)  49.8 us
    add x15, other arithmetic, follow(): return (earlier[0] * later[0], later[0][..., None] * earlier[1] + later[1])  49.1 us
    dynamic_update_slice x8, local copies, waits for them, and re-layouts, compose(): return lax.scan(advance, initial, (decays, own_states), reverse=backward)  21.5 us
    psum x1, blocking collectives, step_on_yards(): return lax.psum(base_arr, lane_axis)  20.6 us
  transfers between devices with their start and end apart: 4, of which 3 were waited for; matrix products, arithmetic and copies ran while one was open for 18% of the time, Pallas kernels for 0%

profile of v1, /device:TPU:0, one launch (start us, length us, event | category | flops | bytes accessed | tf_op | source)
XLA Modules:
  0.0 640.1 jit_solution(8597746479509713004)
XLA Ops:
  19.8 2.9 reshape.128
  22.7 3.2 copy.93
  26.0 2.6 reshape.124
  28.6 5.5 fusion.57
  35.9 17.7 %while.66 = (s32[]{:T(128)}, f32[40,64]{1,0:T(8,128)S(1)}, f32[40,64,64]{2,1,0:T(8,128)}, f32[2,40,64]{2,1,0:T(8,128)S(1)}, f32[2,40,64,64]{2,3,1,0:T(8,128)}, /...) while((s32[]{:T(128)}, f32[40,64]{1,0:T(8,128)S(1)}, ...), condition=%wide.region_3.4_spmd.clone, body=%wide.region_2.3_spmd.clone.sunk | while | flops 499203 | bytes 6646389 | solution.py:62
  36.0 3.2 select_bitcast_fusion.4
  39.2 2.9 copy.180
  44.6 3.6 select_bitcast_fusion.4
  48.2 2.9 copy.180
  53.9 3.3 copy.90
  57.2 2.7 reshape.125
  59.9 2.8 reshape.127
  62.7 3.5 copy.91
  66.2 7.0 %fusion.50 = f32[2,40,64,64]{2,3,1,0:T(8,128)} fusion(f32[2,64,40,64]{1,3,2,0:T(8,128)} %copy.91, bf16[2,64,40,64]{3,2,1,0:T(8,128)(2,1)} %reshape.125, f32[2,64,40,64]{1,3,2,0:T(8,128)S(1)} %copy.89, f32[2,64,40,64]{1,3,2,0:T(8,128)} %copy.90), kind=kOutput, calls=%fused_computation.85 | convolution fusion | flops 252313600 | bytes 5898240 | tf_op jit(solution)/shard_map/nchk,nchv->nhkv/dot_general | solution.py:29
  75.7 29.7 %while.67 = (s32[]{:T(128)}, f32[40,64]{1,0:T(8,128)S(1)}, f32[40,64,64]{2,1,0:T(8,128)}, f32[2,40,64]{2,1,0:T(8,128)}, f32[2,40,64,64]{2,3,1,0:T(8,128)}, /*ind...) while((s32[]{:T(128)}, f32[40,64]{1,0:T(8,128)S(1)}, ...), condition=%wide.region_8.9_spmd.clone, body=%wide.region_7.8_spmd.clone.sunk | while | flops 499204 | bytes 9257093 | solution.py:62
  76.3 2.7 constant_dynamic-slice_fusion.4
  78.9 2.8 copy.181
  81.7 3.2 select_bitcast_fusion.5
  85.0 2.8 copy.182
  93.5 2.8 copy.181
  96.3 3.6 select_bitcast_fusion.5
  99.9 2.8 copy.182
  106.2 27.9 %all-gather = f32[640,64]{1,0:T(8,128)} all-gather(f32[40,64]{1,0:T(8,128)S(1)} %get-tuple-element.322), channel_id=2, replica_groups=mesh['seq'=16,'dp'=2] {'seq'}, dimensions={0}, use_global_device_ids=true | all-gather | bytes 174080 | tf_op jit(solution)/shard_map/all_gather | solution.py:16
  134.1 21.9 %all-gather.2 = f32[640,64]{1,0:T(8,128)} all-gather(f32[40,64]{1,0:T(8,128)S(1)} %get-tuple-element.327), channel_id=4, replica_groups=mesh['seq'=16,'dp'=2] {'seq'}, dimensions={0}, use_global_device_ids=true | all-gather | bytes 174080 | tf_op jit(solution)/shard_map/all_gather | solution.py:16
  156.0 3.2 fusion.5
  161.6 9.6 %all-gather.7.cloned.1.call-done = f32[640,64,64]{2,1,0:T(8,128)} async-done(((f32[40,64,64]{2,1,0:T(8,128)}), f32[640,64,64]{2,1,0:T(8,128)}) %all-gather.7.cloned.1.call-update) | async-done | bytes 10485776 | tf_op jit(solution)/shard_map/all_gather | solution.py:16
  172.4 2.8 copy.103
  175.3 106.6 %all-gather.9.cloned.1.call-done = f32[640,64,64]{2,1,0:T(8,128)} async-done(((f32[40,64,64]{2,1,0:T(8,128)}), f32[640,64,64]{2,1,0:T(8,128)}) %all-gather.9.cloned.1.call-update) | async-done | bytes 10485776 | tf_op jit(solution)/shard_map/all_gather | solution.py:16
  283.1 60.2 %while.65 = (s32[]{:T(128)}, f32[40,64,64]{2,1,0:T(8,128)}, s32[]{:T(128)}, f32[16,40,64]{2,1,0:T(8,128)}, f32[16,40,64,64]{3,2,1,0:T(8,128)}, /*index=5*/s32[]{:T(128)}, s32[]{:T(128)}, s32[]{:T(128)}, s32[]{:T(128)}) while((s32[]{:T(128)}, f32[40,64,64]{2,1,0:T(8,128)}, s32[]{:T(128)}, f32[16,40,64]{2,1,0:T(8,128)}, ...), condition=%wide.region_10.11_spmd, body=%wide.region_9.10_spmd.sunk | while | flops 327686 | bytes 1996947 | solution.py:25
  283.8 3.3 bitcast_add_fusion.8
  287.8 3.3 bitcast_add_fusion.8
  291.8 3.3 bitcast_add_fusion.8
  295.8 3.3 bitcast_add_fusion.8
  299.8 3.3 bitcast_add_fusion.8
  303.8 3.3 bitcast_add_fusion.8
  307.8 3.3 bitcast_add_fusion.8
  311.8 3.3 bitcast_add_fusion.8
  315.8 3.3 bitcast_add_fusion.8
  319.8 3.3 bitcast_add_fusion.8
  323.8 3.3 bitcast_add_fusion.8
  327.8 3.3 bitcast_add_fusion.8
  331.8 3.3 bitcast_add_fusion.8
  335.8 3.3 bitcast_add_fusion.8
  339.8 3.3 bitcast_add_fusion.8
  343.3 2.8 copy.119
  346.1 6.4 %fusion.24 = f32[2,40,64,64]{3,2,1,0:T(8,128)} fusion(f32[2,40,64,64]{2,3,1,0:T(8,128)} %get-tuple-element.330, f32[40,64,64]{1,2,0:T(8,128)} %copy.119, f32[2,40,64]{2,1,0:T(8,128)S(1)} %copy-done.21, bf16[2,64,40,64]{3,2,1,0:T(8,128)(2,1)} %reshape.124), kind=kOutput, calls=%fused_computation.64 | convolution fusion | flops 252313600 | bytes 3952640 | tf_op jit(solution)/shard_map/nhkv,nthv->nthk/dot_general | solution.py:29
  352.6 4.1 multiply_reduce_fusion
  360.0 6.8 %fusion.9 = f32[2,64,40,64]{1,3,2,0:T(8,128)} fusion(f32[2,40,64,64]{3,2,1,0:T(8,128)S(1)} %fusion.21, f32[2,40,64,64]{3,2,1,0:T(8,128)S(1)} %copy-done.15, f32[2,40,64]{2,1,0:T(8,128)S(1)} %get-tuple-element.498, pred[64,64]{1,0:T(8,128)(4,1)S(1)} %iota_compare_fusion, f32[2,64,40,64]{1,3,2,0:T(8,128)S(1)} %copy-done.2, f32[2,64,40,64]{1,3,2,0:T(8,128)S(1)} %copy.89, ...), kind=kOutput, calls=%fused_computation.36 | convolution fusion | flops 254279680 | bytes 7888896 | tf_op jit(solution)/shard_map/nhts,nshk->nthk/dot_general | solution.py:29
  366.8 11.1 %multiply_subtract_fusion = (f32[2,64,40,64]{1,3,2,0:T(8,128)}, f32[2,64,40,64]{1,3,2,0:T(8,128)}, bf16[2,64,40,64]{1,3,2,0:T(8,128)(2,1)}, bf16[2,64,40,64]{1,3,2,0:T(8,128)(2,1)}, f32[2,64,40]{1,2,0:T(8,128)}) fusion(f32[2,64,40,64]{1,3,2,0:T(8,128)S(1)} %copy-done.2, f32[2,64,40,64]{1,3,2,0:T(8,128)S(1)} %copy-done.3, f32[2,64,40,64]{1,3,2,0:T(8,128)} %fusion.9, ...), kind=kOutput, calls=%fused_computation.39 | convolution fusion | flops 258862080 | bytes 13203456 | tf_op jit(solution)/shard_map/nhst,nshk->nthk/dot_general | solution.py:29
  377.8 3.3 copy.131
  381.1 3.4 fusion.83
  384.5 3.3 copy.132
  387.8 4.9 subtract_subtract_fusion
  392.7 3.2 copy.133
  395.9 2.9 reshape.126
  406.6 3.1 mul.285
  411.6 91.0 %all-reduce.7.cloned.1.call-done = (f32[2560,128]{0,1:T(8,128)}, f32[2560,128]{1,0:T(8,128)}) async-done(((f32[2560,128]{0,1:T(8,128)}, f32[2560,128]{1,0:T(8,128)}), (f32[2560,128]{0,1:T(8,128)}, f32[2560,128]{1,0:T(8,128)})) %all-reduce.7.cloned.1.call-update) | async-done | bytes 2621456 | tf_op jit(solution)/shard_map/psum | solution.py:251
  502.6 9.3 %fusion.52 = f32[2,40,64,64]{3,2,1,0:T(8,128)} fusion(f32[2,64,40,64]{1,3,2,0:T(8,128)} %copy.93, f32[2,64,40,64]{1,3,2,0:T(8,128)S(1)} %copy.89, f32[2,40,64]{2,1,0:T(8,128)S(1)} %get-tuple-element.498, f32[2,64,40,64]{1,3,2,0:T(8,128)} %copy.91, f32[2,64,40,64]{1,3,2,0:T(8,128)} %copy.90), kind=kOutput, calls=%fused_computation.86 | convolution fusion | flops 253296640 | bytes 6574080 | tf_op jit(solution)/shard_map/nthk,nshk->nhts/dot_general | solution.py:29
  511.9 58.1 %all-reduce = (f32[2560]{0:T(1024)S(1)}, f32[2560]{0:T(1024)S(1)}) all-reduce(f32[2560]{0:T(1024)S(1)} %get-tuple-element.496, f32[2560]{0:T(1024)S(1)} %multiply_reduce_fusion.2), channel_id=1, replica_groups=mesh['seq'=16,'dp'=2] {'seq'}, use_global_device_ids=true, to_apply=%region_18.19 | all-reduce | flops 5120 | bytes 40960 | tf_op jit(solution)/shard_map/psum | solution.py:251
  570.0 20.6 %all-reduce.2 = (f32[2560]{0:T(1024)S(1)}, f32[2560]{0:T(1024)S(1)}) all-reduce(f32[2560]{0:T(1024)S(1)} %get-tuple-element.475, f32[2560]{0:T(1024)S(1)} %get-tuple-element.476), channel_id=1, replica_groups=mesh['seq'=16,'dp'=2] {'dp'}, use_global_device_ids=true, to_apply=%region_19.20 | all-reduce | flops 5120 | bytes 40960 | tf_op jit(solution)/shard_map/psum | solution.py:252
  592.0 8.3 %fusion.23 = f32[2,40,64,64]{2,3,1,0:T(8,128)S(1)} fusion(f32[2,40,64,64]{2,3,1,0:T(8,128)} %get-tuple-element.330, f32[40,64,64]{1,2,0:T(8,128)} %copy.119, f32[2,40,64]{2,1,0:T(8,128)S(1)} %copy-done.22, f32[2,64,40,64]{1,3,2,0:T(8,128)} %copy.93, f32[2,64,40,64]{1,3,2,0:T(8,128)S(1)} %copy.89, f32[2,40,64]{2,1,0:T(8,128)S(1)} %copy-done.20), kind=kOutput, calls=%fused_computation.63 | convolution fusion | flops 252968960 | bytes 5939200 | tf_op jit(solution)/shard_map/nthk,nhkv->nthv/dot_general | solution.py:29
  600.3 3.0 fusion.7
  605.2 2.8 convert_element_type.122
  608.0 8.7 %fusion.22 = f32[2,40,64,64]{2,3,1,0:T(8,128)S(1)} fusion(f32[2,40,64,64]{2,3,1,0:T(8,128)} %get-tuple-element.325, f32[40,64,64]{1,2,0:T(8,128)} %copy.103, f32[2,40,64]{2,1,0:T(8,128)S(1)} %get-tuple-element.321, f32[2,64,40,64]{1,3,2,0:T(8,128)} %copy.91, f32[2,64,40,64]{1,3,2,0:T(8,128)S(1)} %copy.89, f32[2,64,40,64]{1,3,2,0:T(8,128)} %copy.90), kind=kOutput, calls=%fused_computation.62 | convolution fusion | flops 252968960 | bytes 7229440 | tf_op jit(solution)/shard_map/nthk,nhkv->nthv/dot_general | solution.py:29
  (137 shorter events, 80.5 us)
Async XLA Ops:
  7.2 2.4 copy-start
  7.2 164.0 %all-gather.7.cloned.1.call-start = ((), (), s32[]{:S(2)}) async-start(), calls=%async_computation | async-start | bytes 22282240 | tf_op jit(solution)/shard_map/all_gather | solution.py:16
  12.8 1.5 copy-start.12
  19.0 9.6 %copy-start.19 = (f32[2,40,64]{2,1,0:T(8,128)}, f32[2,40,64]{2,1,0:T(8,128)S(1)}, u32[]{:S(2)}) copy-start(f32[2,40,64]{2,1,0:T(8,128)S(1)} %get-tuple-element.499) | copy-start | bytes 61444
  53.7 228.2 %all-gather.9.cloned.1.call-start = ((), (), s32[]{:S(2)}) async-start(), calls=%async_computation.1 | async-start | bytes 22282240 | tf_op jit(solution)/shard_map/all_gather | solution.py:16
  105.4 397.2 %all-reduce.7.cloned.1.call-start = ((), (), s32[]{:S(2)}) async-start(), calls=%async_computation.2 | async-start | bytes 5242880 | tf_op jit(solution)/shard_map/psum | solution.py:251
  106.2 53.0 %copy-start.5 = (bf16[2,64,40,64]{3,2,1,0:T(8,128)(2,1)S(1)}, bf16[2,64,40,64]{3,2,1,0:T(8,128)(2,1)}, u32[]{:S(2)}) copy-start(bf16[2,64,40,64]{3,2,1,0:T(8,128)(2,1)} %reshape.124) | copy-start | bytes 1966084
  106.2 53.0 %copy-start.7 = (bf16[2,64,40,64]{3,2,1,0:T(8,128)(2,1)S(1)}, bf16[2,64,40,64]{3,2,1,0:T(8,128)(2,1)}, u32[]{:S(2)}) copy-start(bf16[2,64,40,64]{3,2,1,0:T(8,128)(2,1)} %reshape.125) | copy-start | bytes 1966084
  343.3 2.8 copy-start.21
  346.1 6.5 %copy-start.4 = (f32[2,40,64,64]{2,3,1,0:T(8,128)S(1)}, f32[2,40,64,64]{2,3,1,0:T(8,128)}, u32[]{:S(2)}) copy-start(f32[2,40,64,64]{2,3,1,0:T(8,128)} %get-tuple-element.781) | copy-start | bytes 3932164
  346.1 6.5 %copy-start.10 = (f32[2,40,64,64]{2,3,1,0:T(8,128)S(1)}, f32[2,40,64,64]{2,3,1,0:T(8,128)}, u32[]{:S(2)}) copy-start(f32[2,40,64,64]{2,3,1,0:T(8,128)} %get-tuple-element.325) | copy-start | bytes 3932164
  346.1 6.5 %copy-start.11 = (f32[2,40,64,64]{2,3,1,0:T(8,128)S(1)}, f32[2,40,64,64]{2,3,1,0:T(8,128)}, u32[]{:S(2)}) copy-start(f32[2,40,64,64]{2,3,1,0:T(8,128)} %get-tuple-element.330) | copy-start | bytes 3932164
  352.6 4.1 copy-start.8
  352.6 4.1 copy-start.16
  356.7 2.4 copy-start.1
  356.7 2.5 copy-start.2
  356.7 3.3 copy-start.15
  360.0 6.8 %copy-start.3 = (f32[2,64,40,64]{1,3,2,0:T(8,128)S(1)}, f32[2,64,40,64]{1,3,2,0:T(8,128)}, u32[]{:S(2)}) copy-start(f32[2,64,40,64]{1,3,2,0:T(8,128)} %copy.91) | copy-start | bytes 3932164
  360.0 6.8 %copy-start.20 = (f32[2,40,64]{2,1,0:T(8,128)S(1)}, f32[2,40,64]{2,1,0:T(8,128)}, u32[]{:S(2)}) copy-start(f32[2,40,64]{2,1,0:T(8,128)} %copy-done.19) | copy-start | bytes 61444
  360.0 6.8 %copy-start.23 = (f32[2,64,40]{1,2,0:T(8,128)S(1)}, f32[2,64,40]{1,2,0:T(8,128)}, u32[]{:S(2)}) copy-start(f32[2,64,40]{1,2,0:T(8,128)} %fusion.5) | copy-start | bytes 61444
  398.7 4.3 copy-start.18
  402.4 0.6 copy-start.26
  404.5 225.6 %all-reduce.9.cloned.1.call-start = ((), (), s32[]{:S(2)}) async-start(), calls=%async_computation.3 | async-start | bytes 5242880 | tf_op jit(solution)/shard_map/psum | solution.py:252
  502.6 89.4 %copy-start.22 = (f32[2,40,64]{2,1,0:T(8,128)S(1)}, f32[2,40,64]{2,1,0:T(8,128)}, u32[]{:S(2)}) copy-start(f32[2,40,64]{2,1,0:T(8,128)} %get-tuple-element.326) | copy-start | bytes 61444
  592.0 8.3 %copy-start.9 = (bf16[2,64,40,64]{3,2,1,0:T(8,128)(2,1)S(1)}, bf16[2,64,40,64]{3,2,1,0:T(8,128)(2,1)}, u32[]{:S(2)}) copy-start(bf16[2,64,40,64]{3,2,1,0:T(8,128)(2,1)} %reshape.125) | copy-start | bytes 1966084
  592.0 8.3 %copy-start.13 = (f32[2,40,64,64]{3,2,1,0:T(8,128)S(1)}, f32[2,40,64,64]{3,2,1,0:T(8,128)}, u32[]{:S(2)}) copy-start(f32[2,40,64,64]{3,2,1,0:T(8,128)} %fusion.52) | copy-start | bytes 3932164
  592.0 8.3 %copy-start.24 = (f32[2,64,40]{1,2,0:T(8,128)S(1)}, f32[2,64,40]{1,2,0:T(8,128)}, u32[]{:S(2)}) copy-start(f32[2,64,40]{1,2,0:T(8,128)} %get-tuple-element.495) | copy-start | bytes 61444
  608.0 8.7 %copy-start.6 = (bf16[2,64,40,64]{3,2,1,0:T(8,128)(2,1)S(1)}, bf16[2,64,40,64]{3,2,1,0:T(8,128)(2,1)}, u32[]{:S(2)}) copy-start(bf16[2,64,40,64]{3,2,1,0:T(8,128)(2,1)} %reshape.124) | copy-start | bytes 1966084
  608.0 8.7 %copy-start.14 = (f32[2,40,64,64]{3,2,1,0:T(8,128)S(1)}, f32[2,40,64,64]{3,2,1,0:T(8,128)}, u32[]{:S(2)}) copy-start(f32[2,40,64,64]{3,2,1,0:T(8,128)} %fusion.52) | copy-start | bytes 3932164
  621.6 3.8 copy-start.17
  625.4 2.5 copy-start.27
  630.1 2.3 copy-start.25
Sparse Core Ops, SparseCore 0:
  53.8 117.4 all-gather.6
  172.8 108.9 all-gather.8
  404.7 97.8 all-reduce.6
  504.8 74.4 all-reduce.8
